TPU v7x, 32 devices: a whole 2x2x4 slice. The times are simulated.
32 devices in a mesh: lev: 4 (over z), wav: 8 (over y, x, core).
Axes of the slice: x: 2, y: 2, z: 4, core: 2. Of those that a mesh axis runs over, the one named last changes fastest.
Arguments:
- grid_field: float32 [8, 1216, 1216], P('lev', 'wav'), may hold values from -6 to 6
- truncation_limit: int32 [1216], replicated, may hold values from -1 to 607, as said below
- diffusion_order: int32 [8], P('lev'), may hold values from 1 to 4
- diffusion_strength: float32 [8], P('lev'), may hold values from 2 to 50
- mass_weight: float32 [8], P('lev'), may hold values from 0.25 to 4
Outputs:
- filtered: float32 [8, 1216, 1216], P('lev', 'wav')
- energies: float32 [8], P('lev')
- total_energy: float32 [], replicated
Inputs may be any that keep to these rules, and one draw needn't show every extreme that they name: `truncation_limit`: the largest |wavenumber(q)| kept at index p, with wavenumber(m) = m below 608 and m - 1216 otherwise; the kept set is an ellipse about wavenumber zero; the value at p equals the value at 1216 - p; -1 where nothing is kept; the value at p = 0 is 607.
All inputs are finite; a program needn't handle non-finite values.
Results may differ from a plain program's by a relative error of at most 0.000071.
Values sent between devices are 32-bit elements.
A program may use at most 64 MiB of HBM per device.

v0:
```python
import functools

import jax
import jax.numpy as jnp
import numpy as np
from jax import lax
from jax.experimental import pallas as pl
from jax.experimental.pallas import tpu as pltpu
from jax.sharding import PartitionSpec as P

product_precision = lax.Precision.HIGH


def tables(length):
    step = 32
    coarse = -(-length // step)
    columns = np.arange(length)
    high = 2.0 * np.pi / length * (np.arange(coarse)[:, None] * step * columns[None, :] % length)
    low = 2.0 * np.pi / length * (np.arange(step)[:, None] * columns[None, :] % length)
    cos_high, sin_high = (jnp.asarray(f(high), jnp.float32)[:, None] for f in (np.cos, np.sin))
    cos_low, sin_low = (jnp.asarray(f(low), jnp.float32)[None] for f in (np.cos, np.sin))
    cosine = cos_high * cos_low - sin_high * sin_low
    sine = sin_high * cos_low + cos_high * sin_low
    return tuple(t.reshape(coarse * step, length)[:length] for t in (cosine, sine))


def signed(positions, length):
    return jnp.where(positions < length // 2, positions, positions - length)


def transform(values, cosine_table, sine_table, direction):
    with_cosine = jnp.einsum("scpi,iq->scpq", values, cosine_table, precision=product_precision)
    with_sine = jnp.einsum("scpi,iq->scpq", values, sine_table, precision=product_precision)
    if direction < 0:
        real_part = with_cosine[:, 0] + with_sine[:, 1]
        imaginary = with_cosine[:, 1] - with_sine[:, 0]
    else:
        real_part = with_cosine[:, 0] - with_sine[:, 1]
        imaginary = with_cosine[:, 1] + with_sine[:, 0]
    return jnp.stack([real_part, imaginary], axis=1)


def damping(wave_rows, limits, length, diffusion_order, diffusion_strength):
    wave_first = signed(jnp.arange(length, dtype=jnp.int32), length)
    rows_float = wave_rows.astype(jnp.float32)
    first_float = wave_first.astype(jnp.float32)
    scaled_radius = (rows_float[:, None] ** 2 + first_float[None, :] ** 2) / (0.5 * length) ** 2
    inside = (jnp.abs(wave_first)[None, :] <= limits[:, None]).astype(jnp.float32)
    powered = jnp.power(scaled_radius[None], diffusion_order.astype(jnp.float32)[:, None, None])
    return inside[None] / (1.0 + diffusion_strength[:, None, None] * powered)


def mirrored(values):
    return jnp.roll(jnp.flip(values, -1), 1, -1)


def half_plane(
    grid_field, truncation_limit, diffusion_order, diffusion_strength, cosine_table, sine_table
):
    length = grid_field.shape[2]
    half = length // 2
    row_real = jnp.einsum("sij,jl->sli", grid_field, cosine_table[:, :half], precision=product_precision)
    row_imag = -jnp.einsum("sij,jl->sli", grid_field, sine_table[:, :half], precision=product_precision)
    nyquist = jnp.einsum("sij,j->si", grid_field, cosine_table[:, half], precision=product_precision)
    zero_row = (jnp.arange(half, dtype=jnp.int32) == 0)[None, :, None]
    row_imag = jnp.where(zero_row, nyquist[:, None, :], row_imag)
    along_rows = jnp.stack([row_real, row_imag], axis=1)
    spectrum = transform(
        lax.all_to_all(along_rows, "wav", split_axis=2, concat_axis=3, tiled=True),
        cosine_table,
        sine_table,
        -1,
    )
    column_count = spectrum.shape[2]
    wav_index = lax.axis_index("wav")
    offset = wav_index * column_count
    wave_rows = offset + jnp.arange(column_count, dtype=jnp.int32)
    limits = lax.dynamic_slice(truncation_limit, (offset,), (column_count,))
    damp_main = damping(wave_rows, limits, length, diffusion_order, diffusion_strength)
    nyquist_rows = signed(jnp.full((1,), half, jnp.int32), length)
    damp_top = damping(
        nyquist_rows, truncation_limit[half : half + 1], length, diffusion_order, diffusion_strength
    )[:, 0]
    damped = spectrum * damp_main[:, None]
    packed_real = spectrum[:, 0, 0, :]
    packed_imag = spectrum[:, 1, 0, :]
    back_real = mirrored(packed_real)
    back_imag = mirrored(packed_imag)
    zero_real = (packed_real + back_real) * 0.5 * damp_main[:, 0]
    zero_imag = (packed_imag - back_imag) * 0.5 * damp_main[:, 0]
    top_real = (packed_imag + back_imag) * 0.5 * damp_top
    top_imag = (back_real - packed_real) * 0.5 * damp_top
    is_zero = wave_rows == 0
    column_weight = jnp.where(is_zero, 0.0, 2.0).astype(jnp.float32)
    edge = jnp.sum(zero_real**2 + zero_imag**2 + top_real**2 + top_imag**2, axis=-1)
    main_sum = jnp.sum(damped * damped * column_weight[None, None, :, None], axis=(1, 2, 3))
    partial_value = (main_sum + jnp.where(wav_index == 0, edge, 0.0)) / float(length) ** 4
    zero_column = is_zero[None, :, None]
    repacked = jnp.stack(
        [
            jnp.where(zero_column, (zero_real - top_imag)[:, None, :], damped[:, 0]),
            jnp.where(zero_column, (zero_imag + top_real)[:, None, :], damped[:, 1]),
        ],
        axis=1,
    )
    along_first = transform(repacked, cosine_table, sine_table, 1)
    inverse_area = 1.0 / float(length) ** 2
    received = lax.all_to_all(along_first, "wav", split_axis=3, concat_axis=2, tiled=True)
    row_weight = jnp.where(jnp.arange(half, dtype=jnp.int32) == 0, 1.0, 2.0).astype(jnp.float32)[
        :, None
    ]
    with_cosine = jnp.einsum(
        "spi,pj->sij", received[:, 0] * row_weight, cosine_table[:half], precision=product_precision
    )
    with_sine = jnp.einsum(
        "spi,pj->sij", received[:, 1] * row_weight, sine_table[:half], precision=product_precision
    )
    top_term = received[:, 1, 0, :][:, :, None] * cosine_table[half][None, None, :]
    filtered = (with_cosine - with_sine + top_term) * inverse_area
    return (filtered, partial_value)


LANES = 128
HALF = LANES // 2
MESH = pl.DeviceIdType.MESH


def halves(values):
    high = values.astype(jnp.bfloat16)
    return high, (values - high.astype(jnp.float32)).astype(jnp.bfloat16)


def product(left, right):
    dot = functools.partial(jnp.dot, preferred_element_type=jnp.float32)
    return dot(left[0], right[0]) + dot(left[1], right[0]) + dot(left[0], right[1])


def swap(value):
    count = value.shape[1] // LANES
    turned = [pltpu.roll(value[:, n * LANES : (n + 1) * LANES], HALF, 1) for n in range(count)]
    return jnp.concatenate(turned, 1) if count > 1 else turned[0]


def eight_points(x, sign, signs):
    turn = signs if sign < 0 else -signs

    def four(p, q, r, t):
        a0, a1, a2, a3 = p + r, p - r, q + t, swap(q - t) * turn
        return a0 + a2, a1 + a3, a0 - a2, a1 - a3

    e = four(x[0], x[2], x[4], x[6])
    o = four(x[1], x[3], x[5], x[7])
    root = 0.5**0.5
    odd = (
        o[0],
        root * (o[1] + swap(o[1]) * turn),
        swap(o[2]) * turn,
        root * (swap(o[3]) * turn - o[3]),
    )
    return [e[n] + odd[n] for n in range(4)] + [e[n] - odd[n] for n in range(4)]


def pieces(rows, group_rows, groups):
    found = []
    for group in range(groups):
        start, stop = group * group_rows, min((group + 1) * group_rows, 2 * rows)
        while start < stop:
            part = start // rows
            end = min(stop, (part + 1) * rows)
            found.append((group, start - group * group_rows, part, start - part * rows, end - start))
            start = end
    return found


def fused_kernel(
    sizes,
    grid_ref, limit_ref, order_ref, strength_ref, mass_ref, coarse_ref, fine_ref,
    back_coarse_hbm, back_fine_hbm, twiddle_hbm, base_hbm,
    out_ref, energy_ref, total_ref,
    grid_parts, table, back_table, back_coarse, back_fine, twiddle, base,
    sent_a, got_a, sent_b, got_b, back_a, home_a, back_b, home_b,
    rest, work, damp, energy_mine, energy_all,
    load_sems, send_sems, recv_sems, e_send_sems, e_recv_sems, local_sems,
):
    slabs, rows, length, wav, lev, quarters, columns, padded, tail, groups, group_rows, fine_rows = sizes
    everyone = lev * wav
    half = length // 2
    me = lax.axis_index("wav")
    level = lax.axis_index("lev")
    my_quarter, my_slab = me // slabs, me % slabs
    flat = level * wav + me

    barrier = pltpu.get_barrier_semaphore()

    @pl.loop(1, everyone)
    def _(step):
        target = (flat + step) % everyone
        pl.semaphore_signal(barrier, inc=1, device_id=(target // wav, target % wav), device_id_type=MESH)

    loads = [
        pltpu.make_async_copy(src, dst, load_sems.at[n])
        for n, (src, dst) in enumerate(
            ((twiddle_hbm, twiddle), (base_hbm, base), (back_coarse_hbm, back_coarse), (back_fine_hbm, back_fine))
        )
    ]
    for load in loads:
        load.start()
    high, low = halves(grid_ref[...])
    grid_parts[0] = high
    grid_parts[1] = low

    def quarter_of(step):
        down, across = 1 - step % 2, 1 - step // 2
        y, x = my_quarter // 2, my_quarter % 2
        return (y + down - 2 * y * down) * 2 + (x + across - 2 * x * across)

    def push(source, target, phase, w):
        @pl.when(w != me)
        def _():
            pltpu.make_async_remote_copy(
                src_ref=source.at[w], dst_ref=target.at[me],
                send_sem=send_sems.at[phase, w], recv_sem=recv_sems.at[phase, me],
                device_id=(level, w), device_id_type=MESH,
            ).start()

        @pl.when(w == me)
        def _():
            pltpu.make_async_copy(source.at[w], target.at[w], local_sems.at[phase]).start()

    def arrive(source, target, phase, w):
        @pl.when(w != me)
        def _():
            pltpu.make_async_remote_copy(
                src_ref=source.at[w], dst_ref=target.at[w],
                send_sem=send_sems.at[phase, w], recv_sem=recv_sems.at[phase, w],
                device_id=(level, w), device_id_type=MESH,
            ).wait()

        @pl.when(w == me)
        def _():
            pltpu.make_async_copy(source.at[w], target.at[w], local_sems.at[phase]).wait()

    lane = lax.broadcasted_iota(jnp.int32, (1, LANES), 1)
    signs = jnp.where(lane < HALF, 1.0, -1.0)
    in_part = [(lane >= part * HALF) & (lane < part * HALF + tail) for part in range(2)]
    layout = pieces(rows, group_rows, groups)

    def pack(tile):
        shifted = {}
        for group, at, part, start, count in layout:
            piece = jnp.where(in_part[part], tile(start, count), 0.0)
            shift = (group * tail - part * HALF) % LANES
            shifted.setdefault(group, []).append(pltpu.roll(piece, shift, 1) if shift else piece)
        packed = jnp.zeros((group_rows, LANES), jnp.float32)
        for found in shifted.values():
            whole = jnp.concatenate(found, 0) if len(found) > 1 else found[0]
            if whole.shape[0] < group_rows:
                fill = jnp.zeros((group_rows - whole.shape[0], LANES), jnp.float32)
                whole = jnp.concatenate([whole, fill], 0)
            packed = packed + whole
        return packed

    def unpack(packed):
        found = {0: [], 1: []}
        for group, at, part, start, count in layout:
            piece = packed[at : at + count]
            shift = (part * HALF - group * tail) % LANES
            piece = pltpu.roll(piece, shift, 1) if shift else piece
            found[part].append(jnp.where(in_part[part], piece, 0.0))
        return jnp.concatenate(found[0], 0) + jnp.concatenate(found[1], 0)

    def forward(first, count, phase, source, target):
        @pl.loop(0, quarters)
        def _(step):
            quarter = quarter_of(step)
            columns_of = slice(first * LANES, (first + count) * LANES)
            cos_f, sin_f = fine_ref[0, quarter, :, columns_of], fine_ref[1, quarter, :, columns_of]

            @pl.loop(0, length // fine_rows, unroll=2)
            def _(block):
                cos_c = coarse_ref[0, quarter, pl.ds(block, 1)][:, columns_of]
                sin_c = coarse_ref[1, quarter, pl.ds(block, 1)][:, columns_of]
                span = pl.ds(pl.multiple_of(block * fine_rows, fine_rows), fine_rows)
                value_high, value_low = halves(cos_c * cos_f - sin_c * sin_f)
                table[0, span, : count * LANES] = value_high
                table[1, span, : count * LANES] = value_low

            result = product(
                (grid_parts[0], grid_parts[1]), (table[0, :, : count * LANES], table[1, :, : count * LANES])
            )
            for slab in range(slabs):
                w = quarter * slabs + slab
                source[w, :rows] = result[slab * rows : (slab + 1) * rows, :LANES]
                if count > 1:
                    source[w, rows:] = pack(
                        lambda start, many: result[slab * rows + start : slab * rows + start + many, LANES:]
                    )

            if first == 0:
                @pl.when(step == 0)
                def _():
                    pl.semaphore_wait(barrier, everyone - 1)

            for slab in range(slabs):
                push(source, target, phase, quarter * slabs + slab)

    forward(0, 1, 0, sent_a, got_a)
    forward(1, 2, 1, sent_b, got_b)

    loads[0].wait()
    loads[1].wait()
    place = lax.broadcasted_iota(jnp.int32, (1, 3 * LANES), 1)
    column = place // LANES * HALF + place % HALF
    wave = my_quarter * columns + column
    valid = (column < columns) | ((column == columns) & (wave == half))
    single = (wave == 0) | (wave == half)
    out_weight = jnp.where(single, 1.0, 2.0) / float(length) ** 2
    energy_weight = jnp.where(single, 1.0, 0.5)
    limits = jnp.where(valid, limit_ref[my_quarter], -1)
    order = order_ref[my_slab]
    strength = strength_ref[my_slab]
    wave_square = wave.astype(jnp.float32) ** 2

    @pl.loop(0, wav)
    def _(m):
        row = lax.broadcasted_iota(jnp.int32, (padded, 1), 0)
        q = row * wav + m
        signed_q = jnp.where(q < half, q, q - length)
        radius = (wave_square + signed_q.astype(jnp.float32) ** 2) / (0.5 * length) ** 2
        square = radius * radius
        powered = jnp.where(order >= 3, square, 1.0) * jnp.where(order % 2 == 1, radius, square)
        inside = (jnp.abs(signed_q) <= limits) & (row < rows)
        damp[m] = jnp.where(inside, out_weight / (1.0 + strength * powered), 0.0)
        work[m, rows:] = jnp.zeros((padded - rows, 2 * LANES), jnp.float32)

    base_parts = (base[0], base[1])

    def middle(first, count, phase, got, back, home):
        spans = slice(0, count * LANES)
        all_signs = jnp.concatenate([signs] * count, 1)

        @pl.loop(0, rows // 8)
        def _(block):
            span = pl.ds(pl.multiple_of(block * 8, 8), 8)
            for tile in range(count):
                x = [rest[w, span] if tile else got[w, span] for w in range(wav)]
                for m, value in enumerate(eight_points(x, -1, signs)):
                    work[m, span, tile * LANES : (tile + 1) * LANES] = value

        def one_residue(m, sums):
            cos_t = jnp.concatenate([twiddle[0, m]] * count, 1)
            sin_t = jnp.concatenate([twiddle[1, m]] * count, 1)
            value = work[m, :, spans]
            both = product(base_parts, halves(value * cos_t + swap(value) * sin_t))
            value = both[:padded] + swap(both[padded:]) * all_signs
            value = value * damp[m, :, first * LANES : (first + count) * LANES]
            sums = sums + jnp.sum((value * value).reshape(padded // 8, 8, count * LANES), axis=0)
            both = product(base_parts, halves(value))
            value = both[:padded] - swap(both[padded:]) * all_signs
            work[m, :, spans] = value * cos_t - swap(value) * sin_t
            return sums

        sums = lax.fori_loop(0, wav, one_residue, jnp.zeros((8, count * LANES), jnp.float32), unroll=2)
        sums = sums * energy_weight[:, first * LANES : (first + count) * LANES]

        @pl.loop(0, rows // 8)
        def _(block):
            span = pl.ds(pl.multiple_of(block * 8, 8), 8)
            for tile in range(count):
                v = [work[m, span, tile * LANES : (tile + 1) * LANES] for m in range(wav)]
                for w, value in enumerate(eight_points(v, 1, signs)):
                    if tile:
                        rest[w, span] = value
                    else:
                        back[w, span] = value

        @pl.loop(0, quarters)
        def _(step):
            for slab in range(slabs):
                w = quarter_of(step) * slabs + slab
                if count > 1:
                    back[w, rows:] = pack(lambda start, many: rest[w, start : start + many])
                push(back, home, phase, w)

        return sum(sums[:, n * LANES : (n + 1) * LANES] for n in range(count))

    @pl.loop(0, wav)
    def _(w):
        arrive(sent_a, got_a, 0, w)

    sums = middle(0, 1, 2, got_a, back_a, home_a)

    loads[2].wait()
    loads[3].wait()
    blocks = 3 * LANES // fine_rows

    @pl.loop(0, quarters)
    def _(quarter):
        @pl.loop(0, blocks)
        def _(block):
            at = quarter * blocks + block
            cos_c, sin_c = back_coarse[0, pl.ds(at, 1)], back_coarse[1, pl.ds(at, 1)]
            span = pl.ds(pl.multiple_of(block * fine_rows, fine_rows), fine_rows)
            value_high, value_low = halves(cos_c * back_fine[0] - sin_c * back_fine[1])
            back_table[quarter, 0, span] = value_high
            back_table[quarter, 1, span] = value_low

    out_ref[...] = jnp.zeros_like(out_ref)

    @pl.loop(0, wav)
    def _(w):
        arrive(sent_b, got_b, 1, w)
        rest[w] = unpack(got_b[w, rows:])

    sums = sums + middle(1, 2, 3, got_b, back_b, home_b)
    energy_mine[0] = sums
    energy_mine[1] = sums * mass_ref[my_slab]

    def energy_copy(target_flat, slot):
        return pltpu.make_async_remote_copy(
            src_ref=energy_mine, dst_ref=energy_all.at[slot],
            send_sem=e_send_sems.at[target_flat], recv_sem=e_recv_sems.at[slot],
            device_id=(target_flat // wav, target_flat % wav), device_id_type=MESH,
        )

    @pl.loop(1, everyone)
    def _(step):
        energy_copy((flat + step) % everyone, flat).start()

    own_energy = pltpu.make_async_copy(energy_mine, energy_all.at[flat], local_sems.at[4])
    own_energy.start()

    def finish(first, count, phase, back, home):
        @pl.loop(0, quarters)
        def _(step):
            quarter = quarter_of((step + quarters - 1) % quarters)
            stacked = []
            for slab in range(slabs):
                w = quarter * slabs + slab
                arrive(back, home, phase, w)
                tiles = [home[w, :rows]]
                if count > 1:
                    tiles.append(unpack(home[w, rows:]))
                stacked.append(jnp.concatenate(tiles, 1) if count > 1 else tiles[0])
            left = halves(jnp.concatenate(stacked, 0))
            span = slice(first * LANES, (first + count) * LANES)
            out_ref[...] += product(left, (back_table[quarter, 0, span], back_table[quarter, 1, span]))

    finish(0, 1, 2, back_a, home_a)
    finish(1, 2, 3, back_b, home_b)
    own_energy.wait()

    @pl.loop(1, everyone)
    def _(step):
        source = (flat + step) % everyone
        energy_copy(source, source).wait()

    total = energy_all[0, 1]
    for n in range(1, everyone):
        total = total + energy_all[n, 1]
    total_ref[0] = jnp.sum(total) / (lev * slabs)
    for slab in range(slabs):
        tile = energy_all[level * wav + slab, 0]
        for quarter in range(1, quarters):
            tile = tile + energy_all[level * wav + quarter * slabs + slab, 0]
        energy_ref[slab] = jnp.sum(tile)


def cos_sin(phases, length):
    angles = 2.0 * np.pi / length * (phases % length)
    return np.stack([np.cos(angles), np.sin(angles)])


def fused(grid_field, truncation_limit, diffusion_order, diffusion_strength, mass_weight):
    slabs, rows, length = grid_field.shape
    wav, lev = lax.axis_size("wav"), lax.axis_size("lev")
    quarters = wav // slabs
    columns = length // 2 // quarters
    tail = columns + 1 - LANES
    groups = LANES // tail
    group_rows = -(-(-(-2 * rows // groups)) // 8) * 8
    padded = -(-rows // 16) * 16
    fine_rows = 32
    sizes = (slabs, rows, length, wav, lev, quarters, columns, padded, tail, groups, group_rows, fine_rows)
    starts = np.arange(quarters) * columns
    place = np.arange(3 * LANES)
    column = place // LANES * HALF + place % HALF
    phase = (place % LANES >= HALF) * (length // 4)
    waves = starts[:, None] + column[None]
    steps = np.arange(length // fine_rows) * fine_rows
    near = np.arange(fine_rows)
    positions = np.arange(length)
    single = lambda array: jnp.asarray(array, jnp.float32)
    coarse = single(cos_sin(steps[None, :, None] * waves[:, None, :], length))
    fine = single(cos_sin(near[None, :, None] * waves[:, None, :] + phase, length))
    back_starts = waves[:, ::fine_rows].reshape(-1)
    back_phase = np.tile(phase[::fine_rows], quarters)
    back_coarse = single(cos_sin(back_starts[:, None] * positions[None] + back_phase[:, None], length))
    back_fine = single(cos_sin(near[:, None] * positions[None], length))
    inner = np.arange(padded)
    spread = np.zeros((1, 1, LANES), np.int64)
    twiddle = cos_sin(np.arange(wav)[:, None, None] * inner[None, :, None] + spread, length)
    twiddle[1] *= np.where(np.arange(LANES) < HALF, 1.0, -1.0)
    twiddle = single(twiddle)
    base_exact = cos_sin(wav * inner[:, None] * inner[None], length)
    base_exact = base_exact * ((inner[:, None] < rows) & (inner[None] < rows))
    base_exact = base_exact.reshape(2 * padded, padded).astype(np.float32)
    base_high = base_exact.astype(jnp.bfloat16)
    base_low = (base_exact - base_high.astype(np.float32)).astype(jnp.bfloat16)
    base = jnp.asarray(np.stack([base_high, base_low]))
    tiles = [truncation_limit[start : start + HALF] for start in waves[:, ::LANES].reshape(-1).tolist()]
    limits = jnp.concatenate([tile for tile in tiles for _ in range(2)]).reshape(quarters, 1, 3 * LANES)
    chunk_a = pltpu.VMEM((wav, rows, LANES), jnp.float32)
    chunk_b = pltpu.VMEM((wav, rows + group_rows, LANES), jnp.float32)
    everyone = wav * lev
    vmem, smem, anywhere = (pl.BlockSpec(memory_space=m) for m in (pltpu.VMEM, pltpu.SMEM, pl.ANY))
    f32, bf16 = jnp.float32, jnp.bfloat16
    filtered, energies, total = pl.pallas_call(
        functools.partial(fused_kernel, sizes),
        out_shape=(
            jax.ShapeDtypeStruct((slabs * rows, length), f32),
            jax.ShapeDtypeStruct((slabs,), f32),
            jax.ShapeDtypeStruct((1,), f32),
        ),
        in_specs=[vmem, vmem, smem, smem, smem, vmem, vmem] + [anywhere] * 4,
        out_specs=(vmem, smem, smem),
        scratch_shapes=[
            pltpu.VMEM((2, slabs * rows, length), bf16),
            pltpu.VMEM((2, length, 2 * LANES), bf16),
            pltpu.VMEM((quarters, 2, 3 * LANES, length), bf16),
            pltpu.VMEM(back_coarse.shape, f32),
            pltpu.VMEM(back_fine.shape, f32),
            pltpu.VMEM(twiddle.shape, f32),
            pltpu.VMEM(base.shape, bf16),
            chunk_a, chunk_a, chunk_b, chunk_b, chunk_a, chunk_a, chunk_b, chunk_b,
            pltpu.VMEM((wav, rows, LANES), f32),
            pltpu.VMEM((wav, padded, 2 * LANES), f32),
            pltpu.VMEM((wav, padded, 3 * LANES), f32),
            pltpu.VMEM((2, 8, LANES), f32),
            pltpu.VMEM((everyone, 2, 8, LANES), f32),
            pltpu.SemaphoreType.DMA((4,)),
            pltpu.SemaphoreType.DMA((4, wav)),
            pltpu.SemaphoreType.DMA((4, wav)),
            pltpu.SemaphoreType.DMA((everyone,)),
            pltpu.SemaphoreType.DMA((everyone,)),
            pltpu.SemaphoreType.DMA((5,)),
        ],
        compiler_params=pltpu.CompilerParams(
            collective_id=0, has_side_effects=True, vmem_limit_bytes=60 * 1024 * 1024
        ),
        name="fused_step",
    )(
        grid_field.reshape(slabs * rows, length), limits, diffusion_order, diffusion_strength, mass_weight,
        coarse, fine, back_coarse, back_fine, twiddle, base,
    )
    return filtered.reshape(slabs, rows, length), energies, total[0]


def fits(shape):
    slabs, rows, length = shape
    wav = lax.axis_size("wav")
    if wav != 8 or slabs != 2 or rows % 8 or length % 16 or length != rows * wav:
        return False
    columns = length * slabs // 2 // wav
    return length % 32 == 0 and LANES <= columns < LANES + LANES // 2


def local(grid_field, truncation_limit, diffusion_order, diffusion_strength, mass_weight):
    slab_count, row_count, length = grid_field.shape
    if fits(grid_field.shape):
        return fused(
            grid_field, truncation_limit, diffusion_order, diffusion_strength, mass_weight
        )
    cosine_table, sine_table = tables(length)
    filtered, partial_value = half_plane(
        grid_field, truncation_limit, diffusion_order, diffusion_strength, cosine_table, sine_table
    )
    total_slabs = lax.axis_size("lev") * slab_count
    energies = lax.psum(partial_value, "wav")
    weighted_sum = lax.psum(jnp.sum(mass_weight * energies), "lev")
    total_energy = weighted_sum / total_slabs
    return (filtered, energies, total_energy)


def solution(mesh):
    placed = (P("lev", "wav", None), P(), P("lev"), P("lev"), P("lev"))
    return jax.shard_map(
        local,
        mesh=mesh,
        in_specs=placed,
        out_specs=(P("lev", "wav", None), P("lev"), P()),
        check_vma=False,
    )
```

profile of v0, /device:TPU:1, one launch (start us, length us, event | category | flops | bytes accessed | tf_op | source)
XLA Modules:
  0.0 70.1 jit_solution(18369204326078226139)
XLA Ops:
  0.6 1.1 %fusion = (s32[64]{0:T(128)S(1)}, s32[64]{0:T(128)S(1)}, s32[64]{0:T(128)S(1)}, s32[64]{0:T(128)S(1)}, s32[64]{0:T(128)S(1)}, /*index=5*/s32[64]{0:T(128)S(1)}, s32[64]{0:T(128)S(1)}, s32[64]{0:T(128)S(1)}) fusion(s32[1216]{0:T(1024)} %param.12), kind=kLoop, calls=%fused_computation | loop fusion | bytes 4096 | tf_op jit(solution)/shard_map/slice | solution.py:511
  1.7 1.1 %fusion.1 = (s32[128]{0:T(128)S(1)}, s32[128]{0:T(128)S(1)}, s32[128]{0:T(128)S(1)}, s32[128]{0:T(128)S(1)}, s32[128]{0:T(128)S(1)}, /*index=5*/s32[128]{0:T(128)S(1)}, s32[128]{0:T(128)S(1)}, s32[128]{0:T(128)S(1)}) fusion(s32[1216]{0:T(1024)} %param.12), kind=kLoop, calls=%fused_computation.1 | loop fusion | bytes 8192 | tf_op jit(solution)/shard_map/slice | solution.py:511
  2.7 0.1 concatenate.4
  2.8 0.6 reshape.16.limit_ref
  3.4 61.8 %fused_step.1 = (f32[304,1216]{1,0:T(8,128)}, f32[2]{0:T(128)}, f32[1]{0:T(128)}) custom-call(f32[304,1216]{1,0:T(8,128)} %bitcast.3, s32[4,1,384]{2,1,0:T(1,128)} %reshape.16.limit_ref, s32[2]{0:T(128)} %order_ref.1, f32[2]{0:T(128)} %strength_ref.1, f32[2]{0:T(128)} %mass_ref.1, f32[2,4,38,384]{3,2,1,0:T(8,128)} %constant.12.clone.coarse_ref, ...), custom_call_target="tpu_custom_call" | custom-call | tf_op jit(solution)/shard_map/fused_step/pallas_call | solution.py:518
  65.3 0.0 copy-start
  65.3 2.6 %copy.17 = f32[2,152,1216]{2,1,0:T(8,128)} copy(f32[2,152,1216]{2,1,0:T(8,128)} %bitcast.4) | data formatting | bytes 2957312
  67.9 0.0 copy-done
  67.9 0.5 copy.18
Async XLA Ops:
  65.3 2.7 %copy-start = (f32[2]{0:T(128)S(1)}, f32[2]{0:T(128)}, u32[]{:S(2)}) copy-start(f32[2]{0:T(128)} %get-tuple-element.29) | copy-start | bytes 28
where the time goes:
time: 70.4 us; the launch traced here: 70.1 us
  Pallas kernels  61.8 us (88%)
  local copies, waits for them, and re-layouts  5.96 us (8%)
  between operations  2.32 us (3%)
    pallas_call x1, Pallas kernels, fused(): pl.pallas_call(functools.partial(fused_kernel, sizes), out_shape=(jax.Sha...  61.8 us
    unnamed x4, local copies, waits for them, and re-layouts  3.16 us
    slice x2, local copies, waits for them, and re-layouts, fused(): truncation_limit[start:start + HALF]  2.11 us

commit v1 on v0

--- a/solution.py
+++ b/solution.py
@@ -316,7 +316,15 @@
     single = (wave == 0) | (wave == half)
     out_weight = jnp.where(single, 1.0, 2.0) / float(length) ** 2
     energy_weight = jnp.where(single, 1.0, 0.5)
-    limits = jnp.where(valid, limit_ref[my_quarter], -1)
+    all_limits = limit_ref[...]
+    limits = jnp.full((1, 3 * LANES), -1, jnp.int32)
+    for quarter in range(quarters):
+        found = []
+        for tile in range(3):
+            start = quarter * columns + tile * HALF
+            found += [all_limits[:, start : start + HALF]] * 2
+        limits = jnp.where(my_quarter == quarter, jnp.concatenate(found, 1), limits)
+    limits = jnp.where(valid, limits, -1)
     order = order_ref[my_slab]
     strength = strength_ref[my_slab]
     wave_square = wave.astype(jnp.float32) ** 2
@@ -334,22 +342,34 @@
         work[m, rows:] = jnp.zeros((padded - rows, 2 * LANES), jnp.float32)
 
     base_parts = (base[0], base[1])
-
-    def middle(first, count, phase, got, back, home):
+    block_rows = 24
+
+    def in_blocks(body):
+        @pl.loop(0, rows // block_rows)
+        def _(block):
+            body(pl.multiple_of(block * block_rows, 8), block_rows)
+
+        if rows % block_rows:
+            body(rows - rows % block_rows, rows % block_rows)
+
+    def middle(first, count, phase, got, back, home, announce):
         spans = slice(0, count * LANES)
         all_signs = jnp.concatenate([signs] * count, 1)
 
-        @pl.loop(0, rows // 8)
-        def _(block):
-            span = pl.ds(pl.multiple_of(block * 8, 8), 8)
+        def split(start, many):
+            span = pl.ds(start, many)
             for tile in range(count):
                 x = [rest[w, span] if tile else got[w, span] for w in range(wav)]
                 for m, value in enumerate(eight_points(x, -1, signs)):
                     work[m, span, tile * LANES : (tile + 1) * LANES] = value
 
+        in_blocks(split)
+
         def one_residue(m, sums):
-            cos_t = jnp.concatenate([twiddle[0, m]] * count, 1)
-            sin_t = jnp.concatenate([twiddle[1, m]] * count, 1)
+            packed_turn = twiddle[m]
+            other_turn = swap(packed_turn)
+            cos_t = jnp.concatenate([jnp.where(lane < HALF, packed_turn, other_turn)] * count, 1)
+            sin_t = jnp.concatenate([jnp.where(lane < HALF, other_turn, -packed_turn)] * count, 1)
             value = work[m, :, spans]
             both = product(base_parts, halves(value * cos_t + swap(value) * sin_t))
             value = both[:padded] + swap(both[padded:]) * all_signs
@@ -360,12 +380,13 @@
             work[m, :, spans] = value * cos_t - swap(value) * sin_t
             return sums
 
-        sums = lax.fori_loop(0, wav, one_residue, jnp.zeros((8, count * LANES), jnp.float32), unroll=2)
+        sums = lax.fori_loop(0, wav, one_residue, jnp.zeros((8, count * LANES), jnp.float32), unroll=4)
         sums = sums * energy_weight[:, first * LANES : (first + count) * LANES]
 
-        @pl.loop(0, rows // 8)
-        def _(block):
-            span = pl.ds(pl.multiple_of(block * 8, 8), 8)
+        announce(sum(sums[:, n * LANES : (n + 1) * LANES] for n in range(count)))
+
+        def join(start, many):
+            span = pl.ds(start, many)
             for tile in range(count):
                 v = [work[m, span, tile * LANES : (tile + 1) * LANES] for m in range(wav)]
                 for w, value in enumerate(eight_points(v, 1, signs)):
@@ -374,6 +395,8 @@
                     else:
                         back[w, span] = value
 
+        in_blocks(join)
+
         @pl.loop(0, quarters)
         def _(step):
             for slab in range(slabs):
@@ -382,13 +405,32 @@
                     back[w, rows:] = pack(lambda start, many: rest[w, start : start + many])
                 push(back, home, phase, w)
 
-        return sum(sums[:, n * LANES : (n + 1) * LANES] for n in range(count))
-
     @pl.loop(0, wav)
     def _(w):
         arrive(sent_a, got_a, 0, w)
 
-    sums = middle(0, 1, 2, got_a, back_a, home_a)
+    def energy_copy(target_flat, slot):
+        return pltpu.make_async_remote_copy(
+            src_ref=energy_mine, dst_ref=energy_all.at[slot],
+            send_sem=e_send_sems.at[target_flat], recv_sem=e_recv_sems.at[slot],
+            device_id=(target_flat // wav, target_flat % wav), device_id_type=MESH,
+        )
+
+    def announce_first(sums):
+        energy_mine[0] = sums
+
+    def announce_last(sums):
+        sums = sums + energy_mine[0]
+        energy_mine[0] = sums
+        energy_mine[1] = sums * mass_ref[my_slab]
+
+        @pl.loop(1, everyone)
+        def _(step):
+            energy_copy((flat + step) % everyone, flat).start()
+
+        pltpu.make_async_copy(energy_mine, energy_all.at[flat], local_sems.at[4]).start()
+
+    middle(0, 1, 2, got_a, back_a, home_a, announce_first)
 
     loads[2].wait()
     loads[3].wait()
@@ -412,23 +454,8 @@
         arrive(sent_b, got_b, 1, w)
         rest[w] = unpack(got_b[w, rows:])
 
-    sums = sums + middle(1, 2, 3, got_b, back_b, home_b)
-    energy_mine[0] = sums
-    energy_mine[1] = sums * mass_ref[my_slab]
-
-    def energy_copy(target_flat, slot):
-        return pltpu.make_async_remote_copy(
-            src_ref=energy_mine, dst_ref=energy_all.at[slot],
-            send_sem=e_send_sems.at[target_flat], recv_sem=e_recv_sems.at[slot],
-            device_id=(target_flat // wav, target_flat % wav), device_id_type=MESH,
-        )
-
-    @pl.loop(1, everyone)
-    def _(step):
-        energy_copy((flat + step) % everyone, flat).start()
-
+    middle(1, 2, 3, got_b, back_b, home_b, announce_last)
     own_energy = pltpu.make_async_copy(energy_mine, energy_all.at[flat], local_sems.at[4])
-    own_energy.start()
 
     def finish(first, count, phase, back, home):
         @pl.loop(0, quarters)
@@ -498,18 +525,15 @@
     back_coarse = single(cos_sin(back_starts[:, None] * positions[None] + back_phase[:, None], length))
     back_fine = single(cos_sin(near[:, None] * positions[None], length))
     inner = np.arange(padded)
-    spread = np.zeros((1, 1, LANES), np.int64)
-    twiddle = cos_sin(np.arange(wav)[:, None, None] * inner[None, :, None] + spread, length)
-    twiddle[1] *= np.where(np.arange(LANES) < HALF, 1.0, -1.0)
-    twiddle = single(twiddle)
+    turns = cos_sin(np.arange(wav)[:, None, None] * inner[None, :, None], length)
+    twiddle = single(np.repeat(turns, HALF, 3).transpose(1, 2, 0, 3).reshape(wav, padded, LANES))
     base_exact = cos_sin(wav * inner[:, None] * inner[None], length)
     base_exact = base_exact * ((inner[:, None] < rows) & (inner[None] < rows))
     base_exact = base_exact.reshape(2 * padded, padded).astype(np.float32)
     base_high = base_exact.astype(jnp.bfloat16)
     base_low = (base_exact - base_high.astype(np.float32)).astype(jnp.bfloat16)
     base = jnp.asarray(np.stack([base_high, base_low]))
-    tiles = [truncation_limit[start : start + HALF] for start in waves[:, ::LANES].reshape(-1).tolist()]
-    limits = jnp.concatenate([tile for tile in tiles for _ in range(2)]).reshape(quarters, 1, 3 * LANES)
+    limits = truncation_limit.reshape(1, length)
     chunk_a = pltpu.VMEM((wav, rows, LANES), jnp.float32)
     chunk_b = pltpu.VMEM((wav, rows + group_rows, LANES), jnp.float32)
     everyone = wav * lev

time: 70.4 us -> 58.6 us (0.83)
  Pallas kernels: 61.8 us -> 51.5 us
  local copies, waits for them, and re-layouts: 5.96 us -> 4.45 us
    pallas_call x1, Pallas kernels: 61.8 us -> 51.5 us  [fused(): pl.pallas_call(functools.partial(fused_kernel, sizes), out_shape=(jax.Sha...]
    slice x2 -> x0, local copies, waits for them, and re-layouts: 2.11 us -> none  [fused(): truncation_limit[start:start + HALF]]
where the time goes in v1:
time: 58.6 us; the launch traced here: 58.3 us
  Pallas kernels  51.5 us (88%)
  local copies, waits for them, and re-layouts  4.45 us (8%)
  between operations  2.41 us (4%)
    pallas_call x1, Pallas kernels, fused(): pl.pallas_call(functools.partial(fused_kernel, sizes), out_shape=(jax.Sha...  51.5 us
    unnamed x4, local copies, waits for them, and re-layouts  3.16 us
    reshape x1, local copies, waits for them, and re-layouts, fused(): limits = truncation_limit.reshape(1, length)  1.29 us

profile of v1, /device:TPU:1, one launch (start us, length us, event | category | flops | bytes accessed | tf_op | source)
XLA Modules:
  0.0 58.3 jit_solution(14593159396573294252)
XLA Ops:
  0.6 1.3 %reshape.16.limit_ref = s32[1,1216]{1,0:T(1,128)} reshape(s32[1216]{0:T(1024)} %param.12) | data formatting | bytes 9728 | tf_op jit(solution)/shard_map/reshape | solution.py:536
  1.9 51.5 %fused_step.1 = (f32[304,1216]{1,0:T(8,128)}, f32[2]{0:T(128)}, f32[1]{0:T(128)}) custom-call(f32[304,1216]{1,0:T(8,128)} %bitcast.3, s32[1,1216]{1,0:T(1,128)} %reshape.16.limit_ref, s32[2]{0:T(128)} %order_ref.1, f32[2]{0:T(128)} %strength_ref.1, f32[2]{0:T(128)} %mass_ref.1, f32[2,4,38,384]{3,2,1,0:T(8,128)} %constant.12.clone.coarse_ref, ...), custom_call_target="tpu_custom_call" | custom-call | tf_op jit(solution)/shard_map/fused_step/pallas_call | solution.py:542
  53.4 0.0 copy-start
  53.4 2.6 %copy.17 = f32[2,152,1216]{2,1,0:T(8,128)} copy(f32[2,152,1216]{2,1,0:T(8,128)} %bitcast.4) | data formatting | bytes 2957312
  56.1 0.0 copy-done
  56.1 0.5 copy.18
Async XLA Ops:
  53.4 2.7 %copy-start = (f32[2]{0:T(128)S(1)}, f32[2]{0:T(128)}, u32[]{:S(2)}) copy-start(f32[2]{0:T(128)} %get-tuple-element.13) | copy-start | bytes 28

commit v2 on v1

--- a/solution.py
+++ b/solution.py
@@ -341,7 +341,11 @@
         damp[m] = jnp.where(inside, out_weight / (1.0 + strength * powered), 0.0)
         work[m, rows:] = jnp.zeros((padded - rows, 2 * LANES), jnp.float32)
 
-    base_parts = (base[0], base[1])
+    def along(value):
+        value_high, value_low = halves(value)
+        stacked = jnp.concatenate([value_high, value_high, value_low], 0)
+        return jnp.dot(base[...], stacked, preferred_element_type=jnp.float32)
+
     block_rows = 24
 
     def in_blocks(body):
@@ -371,16 +375,18 @@
             cos_t = jnp.concatenate([jnp.where(lane < HALF, packed_turn, other_turn)] * count, 1)
             sin_t = jnp.concatenate([jnp.where(lane < HALF, other_turn, -packed_turn)] * count, 1)
             value = work[m, :, spans]
-            both = product(base_parts, halves(value * cos_t + swap(value) * sin_t))
+            both = along(value * cos_t + swap(value) * sin_t)
             value = both[:padded] + swap(both[padded:]) * all_signs
             value = value * damp[m, :, first * LANES : (first + count) * LANES]
             sums = sums + jnp.sum((value * value).reshape(padded // 8, 8, count * LANES), axis=0)
-            both = product(base_parts, halves(value))
+            both = along(value)
             value = both[:padded] - swap(both[padded:]) * all_signs
             work[m, :, spans] = value * cos_t - swap(value) * sin_t
             return sums
 
-        sums = lax.fori_loop(0, wav, one_residue, jnp.zeros((8, count * LANES), jnp.float32), unroll=4)
+        sums = jnp.zeros((8, count * LANES), jnp.float32)
+        for m in range(wav):
+            sums = one_residue(m, sums)
         sums = sums * energy_weight[:, first * LANES : (first + count) * LANES]
 
         announce(sum(sums[:, n * LANES : (n + 1) * LANES] for n in range(count)))
@@ -532,7 +538,7 @@
     base_exact = base_exact.reshape(2 * padded, padded).astype(np.float32)
     base_high = base_exact.astype(jnp.bfloat16)
     base_low = (base_exact - base_high.astype(np.float32)).astype(jnp.bfloat16)
-    base = jnp.asarray(np.stack([base_high, base_low]))
+    base = jnp.asarray(np.concatenate([base_high, base_low, base_high], 1))
     limits = truncation_limit.reshape(1, length)
     chunk_a = pltpu.VMEM((wav, rows, LANES), jnp.float32)
     chunk_b = pltpu.VMEM((wav, rows + group_rows, LANES), jnp.float32)

time: 58.6 us -> 57 us (0.973)
  Pallas kernels: 51.5 us -> 49.9 us
    pallas_call x1, Pallas kernels: 51.5 us -> 49.9 us  [fused(): pl.pallas_call(functools.partial(fused_kernel, sizes), out_shape=(jax.Sha...]
where the time goes in v2:
time: 57 us; the launch traced here: 56.7 us
  Pallas kernels  49.9 us (88%)
  local copies, waits for them, and re-layouts  4.45 us (8%)
  between operations  2.41 us (4%)
    pallas_call x1, Pallas kernels, fused(): pl.pallas_call(functools.partial(fused_kernel, sizes), out_shape=(jax.Sha...  49.9 us
    unnamed x4, local copies, waits for them, and re-layouts  3.16 us
    reshape x1, local copies, waits for them, and re-layouts, fused(): limits = truncation_limit.reshape(1, length)  1.29 us

profile of v2, /device:TPU:1, one launch (start us, length us, event | category | flops | bytes accessed | tf_op | source)
XLA Modules:
  0.0 56.7 jit_solution(2404103383467118767)
XLA Ops:
  0.6 1.3 %reshape.16.limit_ref = s32[1,1216]{1,0:T(1,128)} reshape(s32[1216]{0:T(1024)} %param.12) | data formatting | bytes 9728 | tf_op jit(solution)/shard_map/reshape | solution.py:542
  1.9 49.9 %fused_step.1 = (f32[304,1216]{1,0:T(8,128)}, f32[2]{0:T(128)}, f32[1]{0:T(128)}) custom-call(f32[304,1216]{1,0:T(8,128)} %bitcast.3, s32[1,1216]{1,0:T(1,128)} %reshape.16.limit_ref, s32[2]{0:T(128)} %order_ref.1, f32[2]{0:T(128)} %strength_ref.1, f32[2]{0:T(128)} %mass_ref.1, f32[2,4,38,384]{3,2,1,0:T(8,128)} %constant.12.clone.coarse_ref, ...), custom_call_target="tpu_custom_call" | custom-call | tf_op jit(solution)/shard_map/fused_step/pallas_call | solution.py:548
  51.8 0.0 copy-start
  51.8 2.6 %copy.17 = f32[2,152,1216]{2,1,0:T(8,128)} copy(f32[2,152,1216]{2,1,0:T(8,128)} %bitcast.4) | data formatting | bytes 2957312
  54.5 0.0 copy-done
  54.5 0.5 copy.18
Async XLA Ops:
  51.8 2.7 %copy-start = (f32[2]{0:T(128)S(1)}, f32[2]{0:T(128)}, u32[]{:S(2)}) copy-start(f32[2]{0:T(128)} %get-tuple-element.13) | copy-start | bytes 28
